TPU v7x, 32 devices: a whole 2x2x4 slice. The times are simulated.
32 devices in a mesh: dp: 8 (over z, y), tp: 4 (over x, core).
Axes of the slice: x: 2, y: 2, z: 4, core: 2. Of those that a mesh axis runs over, the one named last changes fastest.
Arguments:
- activations: bfloat16 [16, 256, 768], P('dp', 'tp'), may hold values from -6 to 6
- pair_rep: bfloat16 [16, 256, 256, 256], P('dp', 'tp'), may hold values from -6 to 6
- noise_times: float32 [16], P('dp'), may hold values from 0 to 1
- class_ids: int32 [16], P('dp'), may hold values from 0 to 40
- chain_lengths: int32 [16], P('dp'), may hold values from 64 to 256, as said below
- ada_weight: bfloat16 [256, 4608], replicated, may hold values from -0.375 to 0.375
- class_table: bfloat16 [41, 256], replicated, may hold values from -4 to 4
- pair_weight: bfloat16 [12, 256], replicated, may hold values from -0.375 to 0.375
- attn_in: bfloat16 [4, 768, 768], P(None, None, 'tp'), may hold values from -0.21875 to 0.21875
- attn_out: bfloat16 [768, 768], P('tp'), may hold values from -2.5 to 2.5
- ff_in: bfloat16 [2, 768, 3072], P(None, None, 'tp'), may hold values from -0.21875 to 0.21875
- ff_out: bfloat16 [3072, 768], P('tp'), may hold values from -0.109375 to 0.109375
- cotangent: bfloat16 [16, 256, 768], P('dp', 'tp'), may hold values from -6 to 6
Outputs:
- result: bfloat16 [16, 256, 768], P('dp', 'tp')
- grad_inputs: bfloat16 [16, 256, 768], P('dp', 'tp')
- grad_pair: bfloat16 [16, 256, 256, 256], P('dp', 'tp')
- grad_attn_in: float32 [4, 768, 768], P(None, 'dp', 'tp')
- grad_attn_out: float32 [768, 768], P('tp', 'dp')
- grad_ff_in: float32 [2, 768, 3072], P(None, 'dp', 'tp')
- grad_ff_out: float32 [3072, 768], P('tp', 'dp')
- grad_ada: float32 [256, 4608], P(None, 'dp')
- grad_table: float32 [41, 256], P(None, 'dp')
- grad_pair_weight: float32 [12, 256], P(None, 'dp')
Inputs may be any that keep to these rules, and one draw needn't show every extreme that they name: `chain_lengths`: every chain has at least a quarter of its 256 slots valid, and in each draw some chain has all 256.
All inputs are finite; a program needn't handle non-finite values.
Results may differ from a plain program's by a relative error of at most 0.02.
The roundings to bfloat16 on the way count: a program that leaves them out, or rounds other values in their place, can miss the bound.
Values may be sent and summed in bfloat16 or wider, within the bound.
A program may use at most 128 MiB of HBM per device.

v0:
```python
import math
import jax
import jax.numpy as jnp
from jax import lax
from jax.sharding import PartitionSpec as P

highest = lax.Precision.HIGHEST


def time_features(noise_times, cond_width):
    half_width = cond_width // 2
    freq_steps = jnp.arange(half_width).astype(jnp.float32)
    frequency = jnp.exp(freq_steps * (-math.log(10000.0) / half_width))
    angles = 100.0 * noise_times[:, None] * frequency[None, :]
    return jnp.concatenate([jnp.sin(angles), jnp.cos(angles)], axis=1)


def normalize(rows_in):
    centered = rows_in - jnp.mean(rows_in, axis=-1, keepdims=True)
    inverse = lax.rsqrt(jnp.mean(centered * centered, axis=-1, keepdims=True) + 1e-05)
    return (centered * inverse, inverse)


def norm_back(grad_rows, normed, inverse):
    mean_grad = jnp.mean(grad_rows, axis=-1, keepdims=True)
    mean_cross = jnp.mean(grad_rows * normed, axis=-1, keepdims=True)
    return inverse * (grad_rows - mean_grad - normed * mean_cross)


def row_sums(values):
    return jnp.sum(values, axis=1)


def local(
    activations,
    pair_rep,
    noise_times,
    class_ids,
    chain_lengths,
    ada_weight,
    class_table,
    pair_weight,
    attn_in,
    attn_out,
    ff_in,
    ff_out,
    cotangent,
):
    chains, local_rows, width = activations.shape
    length = pair_rep.shape[2]
    heads_here = pair_weight.shape[0] // lax.axis_size("tp")
    head_local = attn_in.shape[2]
    head_width = head_local // heads_here
    score_scale = head_width ** (-0.5)
    head_shape = (chains, length, heads_here, head_width)
    onehot = (class_ids[:, None] == jnp.arange(class_table.shape[0])[None, :]).astype(jnp.float32)
    table_full = class_table.astype(jnp.float32)
    ada_full = ada_weight.astype(jnp.float32)
    condition = time_features(noise_times, class_table.shape[1]) + jnp.dot(
        onehot, table_full, precision=highest
    )
    modulation = jnp.dot(condition, ada_full, precision=highest)
    pieces = [modulation[:, entry * width : (entry + 1) * width][:, None, :] for entry in range(6)]
    scale_attn, shift_attn, gate_attn, scale_ff, shift_ff, gate_ff = pieces
    inputs_full = activations.astype(jnp.float32)
    normed_attn, inverse_attn = normalize(inputs_full)
    rows_attn = (normed_attn * (1.0 + scale_attn) + shift_attn).astype(jnp.bfloat16)
    gathered_attn = lax.all_gather(rows_attn, "tp", axis=1, tiled=True)
    projected = jnp.einsum(
        "gld,kde->kgle", gathered_attn, attn_in, preferred_element_type=jnp.float32
    )
    query = projected[0].astype(jnp.bfloat16).reshape(head_shape)
    key_rows = projected[1].astype(jnp.bfloat16).reshape(head_shape)
    value_rows = projected[2].astype(jnp.bfloat16).reshape(head_shape)
    gate_pre = projected[3]
    bias_local = jnp.einsum(
        "gqkp,hp->ghqk", pair_rep, pair_weight, preferred_element_type=jnp.float32
    ).astype(jnp.bfloat16)
    pair_bias = lax.all_to_all(bias_local, "tp", split_axis=1, concat_axis=2, tiled=True)
    key_valid = (jnp.arange(length)[None, :] < chain_lengths[:, None])[:, None, None, :]

    def masked_scores():
        raw_scores = jnp.einsum(
            "gqhe,gkhe->ghqk", query, key_rows, preferred_element_type=jnp.float32
        ) * score_scale + pair_bias.astype(jnp.float32)
        return jnp.where(key_valid, raw_scores, -1e30)

    scores = masked_scores()
    row_top = jnp.max(scores, axis=-1, keepdims=True)
    log_total = row_top + jnp.log(jnp.sum(jnp.exp(scores - row_top), axis=-1, keepdims=True))
    soft_low = jnp.exp(scores - log_total).astype(jnp.bfloat16)
    head_mix = jnp.einsum(
        "ghqk,gkhe->gqhe", soft_low, value_rows, preferred_element_type=jnp.float32
    ).reshape(chains, length, head_local)
    gate_sig = jax.nn.sigmoid(gate_pre)
    gated_mix = (head_mix * gate_sig).astype(jnp.bfloat16)
    attn_terms = jnp.einsum("gle,ed->gld", gated_mix, attn_out, preferred_element_type=jnp.float32)
    attended = lax.psum_scatter(
        attn_terms.astype(jnp.bfloat16), "tp", scatter_dimension=1, tiled=True
    ).astype(jnp.float32)
    sig_attn = jax.nn.sigmoid(gate_attn)
    middle = inputs_full + sig_attn * attended
    normed_ff, inverse_ff = normalize(middle)
    rows_ff = (normed_ff * (1.0 + scale_ff) + shift_ff).astype(jnp.bfloat16)
    gathered_ff = lax.all_gather(rows_ff, "tp", axis=1, tiled=True)
    gate_up = jnp.einsum("gld,kdf->kglf", gathered_ff, ff_in, preferred_element_type=jnp.float32)
    sig_hidden = jax.nn.sigmoid(gate_up[0])
    silu_hidden = gate_up[0] * sig_hidden
    hidden = (silu_hidden * gate_up[1]).astype(jnp.bfloat16)
    ff_terms = jnp.einsum("glf,fd->gld", hidden, ff_out, preferred_element_type=jnp.float32)
    transition = lax.psum_scatter(
        ff_terms.astype(jnp.bfloat16), "tp", scatter_dimension=1, tiled=True
    ).astype(jnp.float32)
    sig_ff = jax.nn.sigmoid(gate_ff)
    result = (middle + sig_ff * transition).astype(jnp.bfloat16)
    upstream = cotangent.astype(jnp.float32)
    grad_trans = (sig_ff * upstream).astype(jnp.bfloat16)
    grad_gate_ff = row_sums(upstream * transition) * (sig_ff * (1.0 - sig_ff))[:, 0, :]
    gathered_grad_ff = lax.all_gather(grad_trans, "tp", axis=1, tiled=True)
    grad_ff_out = jnp.einsum(
        "glf,gld->fd", hidden, gathered_grad_ff, preferred_element_type=jnp.float32
    )
    grad_hidden = jnp.einsum(
        "gld,fd->glf", gathered_grad_ff, ff_out, preferred_element_type=jnp.float32
    )
    silu_slope = sig_hidden * (1.0 + gate_up[0] * (1.0 - sig_hidden))
    grad_gate_up = jnp.stack(
        [grad_hidden * gate_up[1] * silu_slope, grad_hidden * silu_hidden]
    ).astype(jnp.bfloat16)
    grad_ff_in = jnp.einsum(
        "gld,kglf->kdf", gathered_ff, grad_gate_up, preferred_element_type=jnp.float32
    )
    ff_row_terms = jnp.einsum(
        "kglf,kdf->gld", grad_gate_up, ff_in, preferred_element_type=jnp.float32
    )
    grad_rows_ff = lax.psum_scatter(
        ff_row_terms.astype(jnp.bfloat16), "tp", scatter_dimension=1, tiled=True
    ).astype(jnp.float32)
    grad_scale_ff = row_sums(grad_rows_ff * normed_ff)
    grad_shift_ff = row_sums(grad_rows_ff)
    grad_middle = upstream + norm_back(grad_rows_ff * (1.0 + scale_ff), normed_ff, inverse_ff)
    grad_attended = (sig_attn * grad_middle).astype(jnp.bfloat16)
    grad_gate_attn = row_sums(grad_middle * attended) * (sig_attn * (1.0 - sig_attn))[:, 0, :]
    gathered_grad_attn = lax.all_gather(grad_attended, "tp", axis=1, tiled=True)
    grad_attn_out = jnp.einsum(
        "gle,gld->ed", gated_mix, gathered_grad_attn, preferred_element_type=jnp.float32
    )
    grad_gated = jnp.einsum(
        "gld,ed->gle", gathered_grad_attn, attn_out, preferred_element_type=jnp.float32
    )
    grad_mix = (grad_gated * gate_sig).astype(jnp.bfloat16)
    grad_gate_pre = (grad_gated * head_mix * gate_sig * (1.0 - gate_sig)).astype(jnp.bfloat16)
    grad_mix_heads = grad_mix.reshape(head_shape)
    soft_full = jnp.exp(masked_scores() - log_total)
    grad_soft = jnp.einsum(
        "gqhe,gkhe->ghqk", grad_mix_heads, value_rows, preferred_element_type=jnp.float32
    )
    grad_scores = (
        soft_full * (grad_soft - jnp.sum(grad_soft * soft_full, axis=-1, keepdims=True))
    ).astype(jnp.bfloat16)
    grad_query = (
        jnp.einsum("ghqk,gkhe->gqhe", grad_scores, key_rows, preferred_element_type=jnp.float32)
        * score_scale
    ).astype(jnp.bfloat16)
    grad_key = (
        jnp.einsum("ghqk,gqhe->gkhe", grad_scores, query, preferred_element_type=jnp.float32)
        * score_scale
    ).astype(jnp.bfloat16)
    grad_value = jnp.einsum(
        "ghqk,gqhe->gkhe", soft_low, grad_mix_heads, preferred_element_type=jnp.float32
    ).astype(jnp.bfloat16)
    flat_shape = (chains, length, head_local)
    grad_heads = jnp.stack(
        [
            grad_query.reshape(flat_shape),
            grad_key.reshape(flat_shape),
            grad_value.reshape(flat_shape),
            grad_gate_pre,
        ]
    )
    grad_attn_in = jnp.einsum(
        "gld,kgle->kde", gathered_attn, grad_heads, preferred_element_type=jnp.float32
    )
    attn_row_terms = jnp.einsum(
        "kgle,kde->gld", grad_heads, attn_in, preferred_element_type=jnp.float32
    )
    grad_rows_attn = lax.psum_scatter(
        attn_row_terms.astype(jnp.bfloat16), "tp", scatter_dimension=1, tiled=True
    ).astype(jnp.float32)
    grad_scale_attn = row_sums(grad_rows_attn * normed_attn)
    grad_shift_attn = row_sums(grad_rows_attn)
    grad_inputs = (
        grad_middle + norm_back(grad_rows_attn * (1.0 + scale_attn), normed_attn, inverse_attn)
    ).astype(jnp.bfloat16)
    bias_grads = lax.all_to_all(grad_scores, "tp", split_axis=2, concat_axis=1, tiled=True)
    grad_pair = jnp.einsum(
        "ghqk,hp->gqkp", bias_grads, pair_weight, preferred_element_type=jnp.float32
    ).astype(jnp.bfloat16)
    pair_weight_part = jnp.einsum(
        "gqkp,ghqk->hp", pair_rep, bias_grads, preferred_element_type=jnp.float32
    )
    modulation_part = jnp.concatenate(
        [
            grad_scale_attn,
            grad_shift_attn,
            grad_gate_attn,
            grad_scale_ff,
            grad_shift_ff,
            grad_gate_ff,
        ],
        axis=1,
    )
    grad_modulation, pair_weight_sum = (
        lax.psum(modulation_part.astype(jnp.bfloat16), "tp").astype(jnp.float32),
        lax.psum(pair_weight_part.astype(jnp.bfloat16), "tp").astype(jnp.float32),
    )
    grad_condition = jnp.dot(grad_modulation, ada_full.T, precision=highest)
    parts = lax.axis_size("dp")
    place = lax.axis_index("dp")
    sizes = [ada_full.shape[1], condition.shape[1], condition.shape[1], onehot.shape[1]]
    chain_rows = jnp.concatenate([grad_modulation, grad_condition, condition, onehot], axis=1)
    packed = jnp.concatenate([chain_rows.reshape(-1), pair_weight_sum.reshape(-1)])
    packed = jnp.pad(packed, (0, -packed.size % 1024)).reshape(-1, 128)
    gathered = lax.all_gather(packed, "dp", axis=0, tiled=True).reshape(parts, -1)
    rows_all = gathered[:, : chain_rows.size].reshape(parts * chains, chain_rows.shape[1])
    pair_all = gathered[:, chain_rows.size : chain_rows.size + pair_weight.size].reshape(
        (parts,) + pair_weight.shape
    )
    cuts = [sum(sizes[:entry]) for entry in range(5)]
    mod_all, grad_cond_all, cond_all, onehot_all = [
        rows_all[:, cuts[entry] : cuts[entry + 1]] for entry in range(4)
    ]

    def own_columns(values, axis):
        width_here = values.shape[axis] // parts
        return lax.dynamic_slice_in_dim(values, place * width_here, width_here, axis)

    grad_ada = jnp.dot(cond_all.T, own_columns(mod_all, 1), precision=highest)
    grad_table = jnp.dot(onehot_all.T, own_columns(grad_cond_all, 1), precision=highest)
    grad_pair_weight = jnp.sum(own_columns(pair_all, 2), axis=0)

    def summed_over_chains(values_list, axes):
        pieces, shapes = ([], [])
        for values, axis in zip(values_list, axes):
            split = (
                values.shape[:axis]
                + (parts, values.shape[axis] // parts)
                + values.shape[axis + 1 :]
            )
            moved = jnp.moveaxis(values.astype(jnp.bfloat16).reshape(split), axis, 0)
            shapes.append(moved.shape[1:])
            pieces.append(moved.reshape(parts, -1, 128))
        joined = jnp.concatenate(pieces, axis=1)
        own = lax.psum_scatter(
            joined.reshape(-1, 128), "dp", scatter_dimension=0, tiled=True
        ).astype(jnp.float32)
        results, start = ([], 0)
        for piece, shape in zip(pieces, shapes):
            results.append(own[start : start + piece.shape[1]].reshape(shape))
            start += piece.shape[1]
        return results

    sum_ff_in, sum_ff_out = summed_over_chains([grad_ff_in, grad_ff_out], [1, 1])
    sum_attn_in, sum_attn_out = summed_over_chains([grad_attn_in, grad_attn_out], [1, 1])
    summed = (
        sum_attn_in,
        sum_attn_out,
        sum_ff_in,
        sum_ff_out,
        grad_ada,
        grad_table,
        grad_pair_weight,
    )
    return (result, grad_inputs, grad_pair) + tuple(summed)


def solution(mesh):
    return jax.shard_map(
        local,
        mesh=mesh,
        in_specs=(
            P("dp", "tp", None),
            P("dp", "tp", None, None),
            P("dp"),
            P("dp"),
            P("dp"),
            P(),
            P(),
            P(),
            P(None, None, "tp"),
            P("tp", None),
            P(None, None, "tp"),
            P("tp", None),
            P("dp", "tp", None),
        ),
        out_specs=(
            P("dp", "tp", None),
            P("dp", "tp", None),
            P("dp", "tp", None, None),
            P(None, "dp", "tp"),
            P("tp", "dp"),
            P(None, "dp", "tp"),
            P("tp", "dp"),
            P(None, "dp"),
            P(None, "dp"),
            P(None, "dp"),
        ),
        check_vma=False,
    )
```

profile of v0, /device:TPU:0, one launch (start us, length us, event | category | flops | bytes accessed | tf_op | source)
XLA Modules:
  0.0 354.6 jit_solution(2040315591612026860)
XLA Ops:
  7.2 11.4 %fusion.11 = bf16[2,12,64,256]{3,1,2,0:T(8,128)(2,1)} fusion(bf16[2,64,256,256]{3,2,1,0:T(8,128)(2,1)} %param.14, bf16[12,256]{1,0:T(8,128)(2,1)} %param.20), kind=kOutput, calls=%fused_computation.33 | convolution fusion | flops 201719808 | bytes 17569792 | tf_op jit(solution)/shard_map/gqkp,hp->ghqk/dot_general | solution.py:76
  18.6 2.4 copy.89
  21.0 4.2 %all-to-all-start = ((bf16[2,12,64,256]{3,2,0,1:T(8,128)(2,1)}), bf16[2,12,64,256]{3,2,0,1:T(8,128)(2,1)S(1)}, u32[]{:S(2)}, u32[]{:S(2)}) async-start(bf16[2,12,64,256]{3,2,0,1:T(8,128)(2,1)} %copy.89), calls=%async_computation | async-start | bytes 1572864 | tf_op jit(solution)/shard_map/all_to_all | solution.py:79
  25.9 2.8 fusion.105
  29.5 12.4 %all_gather.15 = bf16[2,256,768]{2,1,0:T(8,128)(2,1)S(1)} all-gather(bf16[2,64,768]{2,1,0:T(8,128)(2,1)S(1)} %fusion.41), channel_id=1, replica_groups=mesh['dp'=8,'tp'=4] {'tp'}, dimensions={1}, use_global_device_ids=true | all-gather | bytes 983040 | tf_op jit(solution)/shard_map/all_gather | solution.py:68
  42.7 1.9 fusion.101
  45.6 1.3 copy.91
  47.0 3.1 copy.92
  50.0 1.9 fusion.102
  53.8 1.1 fusion.62
  55.0 1.3 convolution_convert_fusion.3
  56.4 9.2 %all_gather.17 = bf16[2,256,768]{2,1,0:T(8,128)(2,1)} all-gather(bf16[2,64,768]{2,1,0:T(8,128)(2,1)S(1)} %fusion.56), channel_id=1, replica_groups=mesh['dp'=8,'tp'=4] {'tp'}, dimensions={1}, use_global_device_ids=true | all-gather | bytes 983040 | tf_op jit(solution)/shard_map/all_gather | solution.py:119
  65.6 15.1 %reduce-scatter.7.cloned.1.call-done = bf16[2,64,768]{2,1,0:T(8,128)(2,1)} async-done(((bf16[2,256,768]{2,1,0:T(8,128)(2,1)}), bf16[2,64,768]{2,1,0:T(8,128)(2,1)}) %reduce-scatter.7.cloned.1.call-update) | async-done | bytes 196624 | tf_op jit(solution)/shard_map/reduce_scatter | solution.py:98
  81.8 1.1 multiply_reduce_fusion.1
  84.0 8.0 %all_gather.16 = bf16[2,256,768]{2,1,0:T(8,128)(2,1)S(1)} all-gather(bf16[2,64,768]{2,1,0:T(8,128)(2,1)S(1)} %add_convert_fusion), channel_id=1, replica_groups=mesh['dp'=8,'tp'=4] {'tp'}, dimensions={1}, use_global_device_ids=true | all-gather | bytes 983040 | tf_op jit(solution)/shard_map/all_gather | solution.py:105
  93.0 1.4 fusion.4
  94.5 2.1 fusion.29
  97.8 2.3 bitcast_convert_fusion.4
  100.2 23.8 %reduce-scatter.11.cloned.1.call-done = bf16[2,64,768]{2,1,0:T(8,128)(2,1)} async-done(((bf16[2,256,768]{2,1,0:T(8,128)(2,1)}), bf16[2,64,768]{2,1,0:T(8,128)(2,1)}) %reduce-scatter.11.cloned.1.call-update) | async-done | bytes 196624 | tf_op jit(solution)/shard_map/reduce_scatter | solution.py:136
  124.0 1.2 fusion.35
  125.7 1.1 multiply_convert_fusion.5
  126.9 8.2 %all_gather.18 = bf16[2,256,768]{2,1,0:T(8,128)(2,1)S(1)} all-gather(bf16[2,64,768]{2,1,0:T(8,128)(2,1)S(1)} %multiply_convert_fusion.5), channel_id=1, replica_groups=mesh['dp'=8,'tp'=4] {'tp'}, dimensions={1}, use_global_device_ids=true | all-gather | bytes 983040 | tf_op jit(solution)/shard_map/all_gather | solution.py:144
  135.1 1.7 multiply_convert_fusion.4
  140.5 1.8 bitcast_convert_fusion.3
  142.4 3.3 convolution_convert_fusion.2
  147.1 3.0 fusion.10
  150.2 3.1 reshape.208
  153.3 2.1 copy.102
  155.3 3.3 reshape.209
  158.6 1.2 pad_maximum_fusion.2
  160.1 3.2 bitcast_convert_fusion.1
  163.3 1.8 copy.105
  165.2 3.0 reshape.218
  168.2 2.8 bitcast_convert_fusion
  171.0 1.6 copy.127
  172.6 5.5 %reshape.216 = bf16[8,1152,128]{2,1,0:T(8,128)(2,1)} reshape(bf16[8,2,96,768]{3,2,1,0:T(8,128)(2,1)} %bitcast.210) | data formatting | bytes 4718592 | tf_op jit(solution)/shard_map/reshape | solution.py:252
  178.0 3.7 %pad_maximum_fusion = bf16[8,1728,128]{2,1,0:T(8,128)(2,1)} fusion(bf16[8,576,128]{2,1,0:T(8,128)(2,1)S(1)} %copy-done.7, bf16[8,1152,128]{2,1,0:T(8,128)(2,1)} %reshape.216), kind=kLoop, calls=%fused_computation.2 | loop fusion | flops 7077888 | bytes 7077888 | tf_op jit(solution)/shard_map/concatenate | solution.py:253
  181.8 1.8 copy.98
  183.5 3.5 all-to-all-start.1
  187.2 12.0 %all-to-all-done.1 = bf16[2,3,256,256]{3,0,1,2:T(2,128)(2,1)S(1)} async-done(((bf16[2,3,256,256]{3,0,1,2:T(2,128)(2,1)}), bf16[2,3,256,256]{3,0,1,2:T(2,128)(2,1)S(1)}, u32[]{:S(2)}, u32[]{:S(2)}) %all-to-all-start.1) | async-done | bytes 786464 | tf_op jit(solution)/shard_map/all_to_all | solution.py:195
  199.4 8.3 %fusion.21 = bf16[12,256]{1,0:T(8,128)(2,1)S(1)} fusion(bf16[2,64,256,256]{3,2,1,0:T(8,128)(2,1)} %param.14, bf16[2,12,64,256]{3,2,1,0:T(8,128)(2,1)S(1)} %bitcast.207), kind=kOutput, calls=%fused_computation.48 | convolution fusion | flops 201329664 | bytes 17569792 | tf_op jit(solution)/shard_map/gqkp,ghqk->hp/dot_general | solution.py:199
  207.9 8.6 %convolution_convert_fusion = bf16[2,64,256,256]{3,2,1,0:T(8,128)(2,1)} fusion(bf16[2,12,64,256]{3,2,1,0:T(8,128)(2,1)S(1)} %bitcast.208, bf16[12,256]{1,0:T(8,128)(2,1)S(1)} %copy-done.42), kind=kOutput, calls=%fused_computation | convolution fusion | flops 209715200 | bytes 17569792 | tf_op jit(solution)/shard_map/ghqk,hp->gqkp/dot_general | solution.py:196
  217.6 2.3 fusion.53
  220.0 10.7 %all-reduce.1 = (bf16[3072]{0:T(1024)(128)(2,1)S(1)}, bf16[2,4608]{1,0:T(2,128)(2,1)S(1)}) all-reduce(bf16[3072]{0:T(1024)(128)(2,1)S(1)} %reshape.223, bf16[2,4608]{1,0:T(2,128)(2,1)S(1)} %constant_dynamic-update-slice_fusion), channel_id=1, replica_groups=mesh['dp'=8,'tp'=4] {'tp'}, use_global_device_ids=true, to_apply=%region_24.25 | all-reduce | flops 12288 | bytes 49152 | tf_op jit(solution)/shard_map/psum | solution.py:215
  230.7 2.4 fusion.106
  233.3 32.3 %all_gather.19 = f32[896,128]{1,0:T(8,128)S(1)} all-gather(f32[112,128]{1,0:T(8,128)S(1)} %fusion.73), channel_id=1, replica_groups=mesh['dp'=8,'tp'=4] {'dp'}, dimensions={0}, use_global_device_ids=true | all-gather | bytes 516096 | tf_op jit(solution)/shard_map/all_gather | solution.py:224
  267.6 1.6 fusion.74
  273.6 70.3 %reduce-scatter.17.cloned.1.call-done = bf16[1728,128]{1,0:T(8,128)(2,1)} async-done(((bf16[13824,128]{1,0:T(8,128)(2,1)}), bf16[1728,128]{1,0:T(8,128)(2,1)}) %reduce-scatter.17.cloned.1.call-update) | async-done | bytes 442384 | tf_op jit(solution)/shard_map/reduce_scatter | solution.py:254
  (213 shorter events, 27.3 us)
Async XLA Ops:
  7.2 85.8 %copy-start = (bf16[2,768,768]{2,1,0:T(8,128)(2,1)S(1)}, bf16[2,768,768]{2,1,0:T(8,128)(2,1)}, u32[]{:S(2)}) copy-start(bf16[2,768,768]{2,1,0:T(8,128)(2,1)} %param.23) | copy-start | bytes 7077892
  18.6 6.7 %copy-start.57 = (f32[2]{0:T(128)S(1)}, f32[2]{0:T(128)}, u32[]{:S(2)}) copy-start(f32[2]{0:T(128)} %param.15) | copy-start | bytes 28
  18.6 6.7 %copy-start.4 = (bf16[2,64,768]{2,1,0:T(8,128)(2,1)S(1)}, bf16[2,64,768]{2,1,0:T(8,128)(2,1)}, u32[]{:S(2)}) copy-start(bf16[2,64,768]{2,1,0:T(8,128)(2,1)} %param.13) | copy-start | bytes 589828
  18.6 7.1 %copy-start.56 = (bf16[41,256]{1,0:T(8,128)(2,1)S(1)}, bf16[41,256]{1,0:T(8,128)(2,1)}, u32[]{:S(2)}) copy-start(bf16[41,256]{1,0:T(8,128)(2,1)} %param.19) | copy-start | bytes 62980
  18.6 7.2 %copy-start.59 = (s32[2]{0:T(128)S(1)}, s32[2]{0:T(128)}, u32[]{:S(2)}) copy-start(s32[2]{0:T(128)} %param.16) | copy-start | bytes 28
  21.0 24.4 %all-to-all-start = ((bf16[2,12,64,256]{3,2,0,1:T(8,128)(2,1)}), bf16[2,12,64,256]{3,2,0,1:T(8,128)(2,1)S(1)}, u32[]{:S(2)}, u32[]{:S(2)}) async-start(bf16[2,12,64,256]{3,2,0,1:T(8,128)(2,1)} %copy.89), calls=%async_computation | async-start | bytes 1572864 | tf_op jit(solution)/shard_map/all_to_all | solution.py:79
  25.2 55.5 %reduce-scatter.7.cloned.1.call-start = ((), (), s32[]{:S(2)}) async-start(), calls=%async_computation.8 | async-start | bytes 983040 | tf_op jit(solution)/shard_map/reduce_scatter | solution.py:98
  25.4 4.1 %copy-start.43 = (f32[2,64]{1,0:T(2,128)}, f32[2,64]{1,0:T(2,128)S(1)}, u32[]{:S(2)}) copy-start(f32[2,64]{1,0:T(2,128)S(1)} %broadcast_multiply_fusion.5) | copy-start | bytes 1540
  25.6 16.3 %copy-start.46 = (f32[2,64]{1,0:T(2,128)}, f32[2,64]{1,0:T(2,128)S(1)}, u32[]{:S(2)}) copy-start(f32[2,64]{1,0:T(2,128)S(1)} %add_rsqrt_fusion.1) | copy-start | bytes 1540
  25.9 3.4 copy-start.52
  25.9 16.0 %copy-start.58 = (s32[2]{0:T(128)S(1)}, s32[2]{0:T(128)}, u32[]{:S(2)}) copy-start(s32[2]{0:T(128)} %param.17) | copy-start | bytes 28
  25.9 16.7 %copy-start.23 = (bf16[4,768,192]{1,2,0:T(8,128)(2,1)S(1)}, bf16[4,768,192]{1,2,0:T(8,128)(2,1)}, u32[]{:S(2)}) copy-start(bf16[4,768,192]{1,2,0:T(8,128)(2,1)} %param.21) | copy-start | bytes 3538948
  29.3 12.6 %copy-start.34 = (f32[2,768]{1,0:T(2,128)}, f32[2,768]{1,0:T(2,128)S(1)}, u32[]{:S(2)}) copy-start(f32[2,768]{1,0:T(2,128)S(1)} %get-tuple-element.76) | copy-start | bytes 18436
  45.4 6.8 %copy-start.12 = (bf16[1,2,256,192]{2,3,0,1:T(8,128)(2,1)}, bf16[1,2,256,192]{2,3,0,1:T(8,128)(2,1)S(1)}, u32[]{:S(2)}) copy-start(bf16[1,2,256,192]{2,3,0,1:T(8,128)(2,1)S(1)} %get-tuple-element.70) | copy-start | bytes 589828
  46.9 3.1 copy-start.17
  46.9 3.1 copy-start.19
  47.0 3.1 copy-start.54
  53.1 3.3 copy-start.8
  53.1 3.3 copy-start.36
  55.0 10.6 %copy-start.14 = (bf16[2,256,192]{1,2,0:T(8,128)(2,1)}, bf16[2,256,192]{1,2,0:T(8,128)(2,1)S(1)}, u32[]{:S(2)}) copy-start(bf16[2,256,192]{1,2,0:T(8,128)(2,1)S(1)} %fusion.62) | copy-start | bytes 589828
  56.3 26.7 %copy-start.45 = (f32[2,768]{1,0:T(2,128)S(1)}, f32[2,768]{1,0:T(2,128)}, u32[]{:S(2)}) copy-start(f32[2,768]{1,0:T(2,128)} %get-tuple-element.73) | copy-start | bytes 18436
  56.3 67.7 %reduce-scatter.11.cloned.1.call-start = ((), (), s32[]{:S(2)}) async-start(), calls=%async_computation.10 | async-start | bytes 983040 | tf_op jit(solution)/shard_map/reduce_scatter | solution.py:136
  81.8 43.4 %copy-start.38 = (f32[2,64]{1,0:T(2,128)}, f32[2,64]{1,0:T(2,128)S(1)}, u32[]{:S(2)}) copy-start(f32[2,64]{1,0:T(2,128)S(1)} %broadcast_multiply_fusion.4) | copy-start | bytes 1540
  82.9 42.3 %copy-start.40 = (f32[2,64]{1,0:T(2,128)}, f32[2,64]{1,0:T(2,128)S(1)}, u32[]{:S(2)}) copy-start(f32[2,64]{1,0:T(2,128)S(1)} %add_rsqrt_fusion) | copy-start | bytes 1540
  97.8 26.3 %copy-start.5 = (bf16[2,64,768]{2,1,0:T(8,128)(2,1)S(1)}, bf16[2,64,768]{2,1,0:T(8,128)(2,1)}, u32[]{:S(2)}) copy-start(bf16[2,64,768]{2,1,0:T(8,128)(2,1)} %reduce-scatter.7.cloned.1.call-done) | copy-start | bytes 589828
  100.1 35.0 %copy-start.22 = (f32[2,3,64,256]{3,2,1,0:T(8,128)S(1)}, f32[2,3,64,256]{3,2,1,0:T(8,128)}, u32[]{:S(2)}) copy-start(f32[2,3,64,256]{3,2,1,0:T(8,128)} %copy-done.21) | copy-start | bytes 1179652
  100.1 116.3 %reduce-scatter.13.cloned.1.call-start = ((), (), s32[]{:S(2)}) async-start(), calls=%async_computation.11 | async-start | bytes 983040 | tf_op jit(solution)/shard_map/reduce_scatter | solution.py:187
  136.8 3.1 copy-start.61
  142.3 75.2 %reduce-scatter.9.cloned.1.call-start = ((), (), s32[]{:S(2)}) async-start(), calls=%async_computation.9 | async-start | bytes 983040 | tf_op jit(solution)/shard_map/reduce_scatter | solution.py:111
  142.4 3.4 copy-start.15
  145.7 124.6 %reduce-scatter.15.cloned.1.call-start = ((), (), s32[]{:S(2)}) async-start(), calls=%async_computation.12 | async-start | bytes 1658880 | tf_op jit(solution)/shard_map/reduce_scatter | solution.py:254
  159.8 184.0 %reduce-scatter.17.cloned.1.call-start = ((), (), s32[]{:S(2)}) async-start(), calls=%async_computation.13 | async-start | bytes 3981312 | tf_op jit(solution)/shard_map/reduce_scatter | solution.py:254
  172.6 5.5 %copy-start.7 = (bf16[8,576,128]{2,1,0:T(8,128)(2,1)S(1)}, bf16[8,576,128]{2,1,0:T(8,128)(2,1)}, u32[]{:S(2)}) copy-start(bf16[8,576,128]{2,1,0:T(8,128)(2,1)} %reshape.218) | copy-start | bytes 3538948
  181.7 5.3 %copy-start.60 = (s32[2]{0:T(128)S(1)}, s32[2]{0:T(128)}, u32[]{:S(2)}) copy-start(s32[2]{0:T(128)} %param.16) | copy-start | bytes 28
  181.7 5.4 %copy-start.6 = (bf16[2,64,768]{2,1,0:T(8,128)(2,1)S(1)}, bf16[2,64,768]{2,1,0:T(8,128)(2,1)}, u32[]{:S(2)}) copy-start(bf16[2,64,768]{2,1,0:T(8,128)(2,1)} %reduce-scatter.11.cloned.1.call-done) | copy-start | bytes 589828
  183.5 15.7 %all-to-all-start.1 = ((bf16[2,3,256,256]{3,0,1,2:T(2,128)(2,1)}), bf16[2,3,256,256]{3,0,1,2:T(2,128)(2,1)S(1)}, u32[]{:S(2)}, u32[]{:S(2)}) async-start(bf16[2,3,256,256]{3,0,1,2:T(2,128)(2,1)} %copy.98), calls=%async_computation.5 | async-start | bytes 1572864 | tf_op jit(solution)/shard_map/all_to_all | solution.py:195
  199.4 8.4 %copy-start.42 = (bf16[12,256]{1,0:T(8,128)(2,1)S(1)}, bf16[12,256]{1,0:T(8,128)(2,1)}, u32[]{:S(2)}) copy-start(bf16[12,256]{1,0:T(8,128)(2,1)} %param.20) | copy-start | bytes 18436
  207.8 9.7 %copy-start.9 = (bf16[2,64,768]{2,1,0:T(8,128)(2,1)S(1)}, bf16[2,64,768]{2,1,0:T(8,128)(2,1)}, u32[]{:S(2)}) copy-start(bf16[2,64,768]{2,1,0:T(8,128)(2,1)} %param.25) | copy-start | bytes 589828
  207.8 9.7 %copy-start.35 = (f32[2,768]{1,0:T(2,128)S(1)}, f32[2,768]{1,0:T(2,128)}, u32[]{:S(2)}) copy-start(f32[2,768]{1,0:T(2,128)} %copy-done.34) | copy-start | bytes 18436
  207.8 9.7 %copy-start.37 = (f32[2,768]{1,0:T(2,128)S(1)}, f32[2,768]{1,0:T(2,128)}, u32[]{:S(2)}) copy-start(f32[2,768]{1,0:T(2,128)} %get-tuple-element.72) | copy-start | bytes 18436
  207.8 9.7 %copy-start.39 = (f32[2,64]{1,0:T(2,128)S(1)}, f32[2,64]{1,0:T(2,128)}, u32[]{:S(2)}) copy-start(f32[2,64]{1,0:T(2,128)} %copy-done.38) | copy-start | bytes 1540
  207.8 9.7 %copy-start.41 = (f32[2,64]{1,0:T(2,128)S(1)}, f32[2,64]{1,0:T(2,128)}, u32[]{:S(2)}) copy-start(f32[2,64]{1,0:T(2,128)} %copy-done.40) | copy-start | bytes 1540
  207.8 9.7 %copy-start.44 = (f32[2,64]{1,0:T(2,128)S(1)}, f32[2,64]{1,0:T(2,128)}, u32[]{:S(2)}) copy-start(f32[2,64]{1,0:T(2,128)} %copy-done.43) | copy-start | bytes 1540
  207.9 9.7 %copy-start.47 = (f32[2,64]{1,0:T(2,128)S(1)}, f32[2,64]{1,0:T(2,128)}, u32[]{:S(2)}) copy-start(f32[2,64]{1,0:T(2,128)} %copy-done.46) | copy-start | bytes 1540
  207.9 9.7 %copy-start.49 = (f32[2,64]{1,0:T(2,128)S(1)}, f32[2,64]{1,0:T(2,128)}, u32[]{:S(2)}) copy-start(f32[2,64]{1,0:T(2,128)} %copy-done.48) | copy-start | bytes 1540
  207.9 9.7 %copy-start.51 = (f32[2,64]{1,0:T(2,128)S(1)}, f32[2,64]{1,0:T(2,128)}, u32[]{:S(2)}) copy-start(f32[2,64]{1,0:T(2,128)} %copy-done.50) | copy-start | bytes 1540
  219.9 13.2 %copy-start.53 = (f32[2,256]{1,0:T(2,128)S(1)}, f32[2,256]{1,0:T(2,128)}, u32[]{:S(2)}) copy-start(f32[2,256]{1,0:T(2,128)} %copy-done.52) | copy-start | bytes 6148
  265.7 3.5 copy-start.16
  (24 other events, 39.7 us)
Sparse Core Ops, SparseCore 0:
  56.4 24.2 reduce-scatter.6
  100.2 23.7 reduce-scatter.10
  142.4 23.7 reduce-scatter.12
  168.6 23.7 reduce-scatter.8
  195.8 65.7 reduce-scatter.14
  265.1 78.7 reduce-scatter.16
where the time goes:
time: 356 us; the launch traced here: 355 us
  waiting for transfers between devices  121 us (34%)
  blocking collectives  80.8 us (23%)
  matrix products  65.1 us (18%)
  local copies, waits for them, and re-layouts  44.4 us (12%)
  other arithmetic  19.8 us (6%)
  between operations  15 us (4%)
  starting transfers between devices  8.16 us (2%)
    reduce_scatter x2, waiting for transfers between devices, summed_over_chains(): lax.psum_scatter(joined.reshape(-1, 128), 'dp', scatter_dimension=0, tile...  70.3 us
    all_gather x1, blocking collectives, local(): lax.all_gather(packed, 'dp', axis=0, tiled=True).reshape(parts, -1)  32.3 us
    reduce_scatter x1, waiting for transfers between devices, local(): lax.psum_scatter(ff_row_terms.astype(jnp.bfloat16), 'tp', scatter_dimensi...  23.8 us
    reduce_scatter x1, waiting for transfers between devices, local(): lax.psum_scatter(attn_terms.astype(jnp.bfloat16), 'tp', scatter_dimension...  15.1 us
    all_gather x1, blocking collectives, local(): gathered_attn = lax.all_gather(rows_attn, 'tp', axis=1, tiled=True)  12.4 us
    reshape x4, local copies, waits for them, and re-layouts, summed_over_chains(): pieces.append(moved.reshape(parts, -1, 128))  12.3 us
    all_to_all x1, waiting for transfers between devices, local(): lax.all_to_all(grad_scores, 'tp', split_axis=2, concat_axis=1, tiled=True)  12 us
    dot_general x1, matrix products, local(): jnp.einsum('gqkp,hp->ghqk', pair_rep, pair_weight, preferred_element_type...  11.4 us
  transfers between devices with their start and end apart: 8, of which 4 were waited for; matrix products, arithmetic and copies ran while one was open for 22% of the time, Pallas kernels for 0%

commit v1 on v0

--- a/solution.py
+++ b/solution.py
@@ -5,6 +5,35 @@
 from jax.sharding import PartitionSpec as P
 
 highest = lax.Precision.HIGHEST
+
+
+def review_counts(inputs, ndim_at):
+    inputs = jnp.moveaxis(inputs, 0, ndim_at)
+    m_next = inputs.shape
+    block_now = inputs.reshape(
+        *m_next[:ndim_at], m_next[ndim_at] * m_next[ndim_at + 1], *m_next[ndim_at + 2 :]
+    )
+    return block_now
+
+
+def detail_meshes_all(body, peer_axis):
+    z2 = lax.psum(1, peer_axis)
+    small = lax.axis_index(peer_axis)
+    far_arr, met_up = (z2, small)
+    r2, carry_out = (body[None], 1)
+    while carry_out < far_arr:
+        latest = lax.ppermute(
+            r2, peer_axis, perm=tuple(((p, p ^ carry_out) for p in range(far_arr)))
+        )
+        v_now = met_up & carry_out == 0
+        r2 = jnp.concatenate([jnp.where(v_now, r2, latest), jnp.where(v_now, latest, r2)])
+        carry_out *= 2
+    return r2
+
+
+def stacks_all_make(array_in, my_tile, row_dim):
+    current_value = review_counts(detail_meshes_all(array_in, my_tile), row_dim)
+    return current_value
 
 
 def time_features(noise_times, cond_width):
@@ -102,7 +131,7 @@
     middle = inputs_full + sig_attn * attended
     normed_ff, inverse_ff = normalize(middle)
     rows_ff = (normed_ff * (1.0 + scale_ff) + shift_ff).astype(jnp.bfloat16)
-    gathered_ff = lax.all_gather(rows_ff, "tp", axis=1, tiled=True)
+    gathered_ff = stacks_all_make(rows_ff, "tp", 1)
     gate_up = jnp.einsum("gld,kdf->kglf", gathered_ff, ff_in, preferred_element_type=jnp.float32)
     sig_hidden = jax.nn.sigmoid(gate_up[0])
     silu_hidden = gate_up[0] * sig_hidden

time: 356 us -> 368 us (1.034)
  waiting for transfers between devices: 121 us -> 131 us
    reduce_scatter x1, waiting for transfers between devices: 15.1 us -> 24.3 us  [local(): lax.psum_scatter(attn_terms.astype(jnp.bfloat16), 'tp', scatter_dimension...]
    all_gather x1 -> x0, blocking collectives: 8.02 us -> none  [local(): gathered_ff = lax.all_gather(rows_ff, 'tp', axis=1, tiled=True)]
    all_gather x1, blocking collectives: 9.17 us -> 15.4 us  [local(): gathered_grad_ff = lax.all_gather(grad_trans, 'tp', axis=1, tiled=True)]
    unnamed x133 -> x135, local copies, waits for them, and re-layouts: 6.75 us -> 7.95 us
  transfers between devices with their start and end apart: 8 -> 10, of which waited for: 4 -> 5; matrix products, arithmetic and copies ran while one was open for 22% -> 22% of each run, Pallas kernels for 0% -> 0%
where the time goes in v1:
time: 368 us; the launch traced here: 367 us
  waiting for transfers between devices  131 us (36%)
  blocking collectives  78.6 us (21%)
  matrix products  65.1 us (18%)
  local copies, waits for them, and re-layouts  45.6 us (12%)
  other arithmetic  22.7 us (6%)
  between operations  15 us (4%)
  starting transfers between devices  8.56 us (2%)
    reduce_scatter x2, waiting for transfers between devices, summed_over_chains(): lax.psum_scatter(joined.reshape(-1, 128), 'dp', scatter_dimension=0, tile...  69.9 us
    all_gather x1, blocking collectives, local(): lax.all_gather(packed, 'dp', axis=0, tiled=True).reshape(parts, -1)  32.5 us
    reduce_scatter x1, waiting for transfers between devices, local(): lax.psum_scatter(attn_terms.astype(jnp.bfloat16), 'tp', scatter_dimension...  24.3 us
    reduce_scatter x1, waiting for transfers between devices, local(): lax.psum_scatter(ff_row_terms.astype(jnp.bfloat16), 'tp', scatter_dimensi...  23.3 us
    all_gather x1, blocking collectives, local(): gathered_grad_ff = lax.all_gather(grad_trans, 'tp', axis=1, tiled=True)  15.4 us
    reshape x4, local copies, waits for them, and re-layouts, summed_over_chains(): pieces.append(moved.reshape(parts, -1, 128))  12.2 us
    all_to_all x1, waiting for transfers between devices, local(): lax.all_to_all(grad_scores, 'tp', split_axis=2, concat_axis=1, tiled=True)  12 us
    all_gather x1, blocking collectives, local(): gathered_attn = lax.all_gather(rows_attn, 'tp', axis=1, tiled=True)  11.8 us
  transfers between devices with their start and end apart: 10, of which 5 were waited for; matrix products, arithmetic and copies ran while one was open for 22% of the time, Pallas kernels for 0%

profile of v1, /device:TPU:0, one launch (start us, length us, event | category | flops | bytes accessed | tf_op | source)
XLA Modules:
  0.0 366.7 jit_solution(7462585703910938950)
XLA Ops:
  7.2 11.4 %fusion.11 = bf16[2,12,64,256]{3,1,2,0:T(8,128)(2,1)} fusion(bf16[2,64,256,256]{3,2,1,0:T(8,128)(2,1)} %param.14, bf16[12,256]{1,0:T(8,128)(2,1)} %param.20), kind=kOutput, calls=%fused_computation.33 | convolution fusion | flops 201719808 | bytes 17569792 | tf_op jit(solution)/shard_map/gqkp,hp->ghqk/dot_general | solution.py:105
  18.6 2.4 copy.96
  21.0 4.2 %all-to-all-start = ((bf16[2,12,64,256]{3,2,0,1:T(8,128)(2,1)}), bf16[2,12,64,256]{3,2,0,1:T(8,128)(2,1)S(1)}, u32[]{:S(2)}, u32[]{:S(2)}) async-start(bf16[2,12,64,256]{3,2,0,1:T(8,128)(2,1)} %copy.96), calls=%async_computation | async-start | bytes 1572864 | tf_op jit(solution)/shard_map/all_to_all | solution.py:108
  26.5 2.8 fusion.104
  30.1 11.8 %all_gather.12 = bf16[2,256,768]{2,1,0:T(8,128)(2,1)S(1)} all-gather(bf16[2,64,768]{2,1,0:T(8,128)(2,1)S(1)} %fusion.39), channel_id=1, replica_groups=mesh['dp'=8,'tp'=4] {'tp'}, dimensions={1}, use_global_device_ids=true | all-gather | bytes 983040 | tf_op jit(solution)/shard_map/all_gather | solution.py:97
  42.7 1.9 fusion.100
  45.7 1.3 copy.98
  47.0 3.1 copy.99
  50.1 1.9 fusion.101
  53.9 1.1 fusion.60
  55.7 1.3 convolution_convert_fusion.3
  57.1 24.3 %reduce-scatter.7.cloned.1.call-done = bf16[2,64,768]{2,1,0:T(8,128)(2,1)} async-done(((bf16[2,256,768]{2,1,0:T(8,128)(2,1)}), bf16[2,64,768]{2,1,0:T(8,128)(2,1)}) %reduce-scatter.7.cloned.1.call-update) | async-done | bytes 196624 | tf_op jit(solution)/shard_map/reduce_scatter | solution.py:127
  84.8 1.4 collective-permute-done
  88.1 15.4 %all_gather.13 = bf16[2,256,768]{2,1,0:T(8,128)(2,1)S(1)} all-gather(bf16[2,64,768]{2,1,0:T(8,128)(2,1)S(1)} %fusion.54), channel_id=1, replica_groups=mesh['dp'=8,'tp'=4] {'tp'}, dimensions={1}, use_global_device_ids=true | all-gather | bytes 983040 | tf_op jit(solution)/shard_map/all_gather | solution.py:148
  103.5 1.3 broadcast_select_fusion.1
  105.9 1.4 fusion.4
  107.3 2.2 fusion.27
  110.6 2.3 bitcast_convert_fusion.4
  113.0 23.3 %reduce-scatter.11.cloned.1.call-done = bf16[2,64,768]{2,1,0:T(8,128)(2,1)} async-done(((bf16[2,256,768]{2,1,0:T(8,128)(2,1)}), bf16[2,64,768]{2,1,0:T(8,128)(2,1)}) %reduce-scatter.11.cloned.1.call-update) | async-done | bytes 196624 | tf_op jit(solution)/shard_map/reduce_scatter | solution.py:165
  136.3 1.2 fusion.33
  138.1 1.1 multiply_convert_fusion.5
  139.2 8.2 %all_gather.14 = bf16[2,256,768]{2,1,0:T(8,128)(2,1)S(1)} all-gather(bf16[2,64,768]{2,1,0:T(8,128)(2,1)S(1)} %multiply_convert_fusion.5), channel_id=1, replica_groups=mesh['dp'=8,'tp'=4] {'tp'}, dimensions={1}, use_global_device_ids=true | all-gather | bytes 983040 | tf_op jit(solution)/shard_map/all_gather | solution.py:173
  147.4 1.7 multiply_convert_fusion.4
  152.8 1.8 bitcast_convert_fusion.3
  154.7 3.3 convolution_convert_fusion.2
  159.5 3.1 fusion.10
  162.5 3.1 reshape.212
  165.6 2.1 copy.110
  167.7 3.3 reshape.213
  171.0 1.2 pad_maximum_fusion.2
  172.5 3.2 bitcast_convert_fusion.1
  175.7 1.8 copy.114
  177.5 3.0 reshape.222
  180.5 2.8 bitcast_convert_fusion
  183.3 1.6 copy.138
  184.9 5.4 %reshape.220 = bf16[8,1152,128]{2,1,0:T(8,128)(2,1)} reshape(bf16[8,2,96,768]{3,2,1,0:T(8,128)(2,1)} %bitcast.215) | data formatting | bytes 4718592 | tf_op jit(solution)/shard_map/reshape | solution.py:281
  190.4 3.7 pad_maximum_fusion
  194.1 1.8 copy.106
  195.9 3.5 all-to-all-start.1
  199.5 12.0 %all-to-all-done.1 = bf16[2,3,256,256]{3,0,1,2:T(2,128)(2,1)S(1)} async-done(((bf16[2,3,256,256]{3,0,1,2:T(2,128)(2,1)}), bf16[2,3,256,256]{3,0,1,2:T(2,128)(2,1)S(1)}, u32[]{:S(2)}, u32[]{:S(2)}) %all-to-all-start.1) | async-done | bytes 786464 | tf_op jit(solution)/shard_map/all_to_all | solution.py:224
  211.7 8.3 %fusion.21 = bf16[12,256]{1,0:T(8,128)(2,1)S(1)} fusion(bf16[2,64,256,256]{3,2,1,0:T(8,128)(2,1)} %param.14, bf16[2,12,64,256]{3,2,1,0:T(8,128)(2,1)S(1)} %bitcast.212), kind=kOutput, calls=%fused_computation.48 | convolution fusion | flops 201329664 | bytes 17569792 | tf_op jit(solution)/shard_map/gqkp,ghqk->hp/dot_general | solution.py:228
  220.2 8.6 %convolution_convert_fusion = bf16[2,64,256,256]{3,2,1,0:T(8,128)(2,1)} fusion(bf16[2,12,64,256]{3,2,1,0:T(8,128)(2,1)S(1)} %bitcast.213, bf16[12,256]{1,0:T(8,128)(2,1)S(1)} %copy-done.43), kind=kOutput, calls=%fused_computation | convolution fusion | flops 209715200 | bytes 17569792 | tf_op jit(solution)/shard_map/ghqk,hp->gqkp/dot_general | solution.py:225
  229.9 2.3 fusion.51
  232.3 10.7 %all-reduce.1 = (bf16[3072]{0:T(1024)(128)(2,1)S(1)}, bf16[2,4608]{1,0:T(2,128)(2,1)S(1)}) all-reduce(bf16[3072]{0:T(1024)(128)(2,1)S(1)} %reshape.227, bf16[2,4608]{1,0:T(2,128)(2,1)S(1)} %constant_dynamic-update-slice_fusion), channel_id=1, replica_groups=mesh['dp'=8,'tp'=4] {'tp'}, use_global_device_ids=true, to_apply=%region_24.25 | all-reduce | flops 12288 | bytes 49152 | tf_op jit(solution)/shard_map/psum | solution.py:244
  243.0 2.4 fusion.105
  245.6 32.5 %all_gather.15 = f32[896,128]{1,0:T(8,128)S(1)} all-gather(f32[112,128]{1,0:T(8,128)S(1)} %fusion.72), channel_id=1, replica_groups=mesh['dp'=8,'tp'=4] {'dp'}, dimensions={0}, use_global_device_ids=true | all-gather | bytes 516096 | tf_op jit(solution)/shard_map/all_gather | solution.py:253
  280.1 1.6 fusion.73
  286.1 69.9 %reduce-scatter.17.cloned.1.call-done = bf16[1728,128]{1,0:T(8,128)(2,1)} async-done(((bf16[13824,128]{1,0:T(8,128)(2,1)}), bf16[1728,128]{1,0:T(8,128)(2,1)}) %reduce-scatter.17.cloned.1.call-update) | async-done | bytes 442384 | tf_op jit(solution)/shard_map/reduce_scatter | solution.py:283
  (223 shorter events, 31.7 us)
Async XLA Ops:
  7.2 98.7 %copy-start = (bf16[2,768,768]{2,1,0:T(8,128)(2,1)S(1)}, bf16[2,768,768]{2,1,0:T(8,128)(2,1)}, u32[]{:S(2)}) copy-start(bf16[2,768,768]{2,1,0:T(8,128)(2,1)} %param.23) | copy-start | bytes 7077892
  18.6 6.7 %copy-start.58 = (f32[2]{0:T(128)S(1)}, f32[2]{0:T(128)}, u32[]{:S(2)}) copy-start(f32[2]{0:T(128)} %param.15) | copy-start | bytes 28
  18.6 6.7 %copy-start.4 = (bf16[2,64,768]{2,1,0:T(8,128)(2,1)S(1)}, bf16[2,64,768]{2,1,0:T(8,128)(2,1)}, u32[]{:S(2)}) copy-start(bf16[2,64,768]{2,1,0:T(8,128)(2,1)} %param.13) | copy-start | bytes 589828
  18.6 7.2 %copy-start.57 = (bf16[41,256]{1,0:T(8,128)(2,1)S(1)}, bf16[41,256]{1,0:T(8,128)(2,1)}, u32[]{:S(2)}) copy-start(bf16[41,256]{1,0:T(8,128)(2,1)} %param.19) | copy-start | bytes 62980
  18.6 7.2 %copy-start.60 = (s32[2]{0:T(128)S(1)}, s32[2]{0:T(128)}, u32[]{:S(2)}) copy-start(s32[2]{0:T(128)} %param.16) | copy-start | bytes 28
  21.0 24.4 %all-to-all-start = ((bf16[2,12,64,256]{3,2,0,1:T(8,128)(2,1)}), bf16[2,12,64,256]{3,2,0,1:T(8,128)(2,1)S(1)}, u32[]{:S(2)}, u32[]{:S(2)}) async-start(bf16[2,12,64,256]{3,2,0,1:T(8,128)(2,1)} %copy.96), calls=%async_computation | async-start | bytes 1572864 | tf_op jit(solution)/shard_map/all_to_all | solution.py:108
  25.2 56.2 %reduce-scatter.7.cloned.1.call-start = ((), (), s32[]{:S(2)}) async-start(), calls=%async_computation.8 | async-start | bytes 983040 | tf_op jit(solution)/shard_map/reduce_scatter | solution.py:127
  25.4 4.7 %copy-start.44 = (f32[2,64]{1,0:T(2,128)}, f32[2,64]{1,0:T(2,128)S(1)}, u32[]{:S(2)}) copy-start(f32[2,64]{1,0:T(2,128)S(1)} %broadcast_multiply_fusion.5) | copy-start | bytes 1540
  25.6 16.3 %copy-start.47 = (f32[2,64]{1,0:T(2,128)}, f32[2,64]{1,0:T(2,128)S(1)}, u32[]{:S(2)}) copy-start(f32[2,64]{1,0:T(2,128)S(1)} %add_rsqrt_fusion.1) | copy-start | bytes 1540
  26.5 15.4 %copy-start.59 = (s32[2]{0:T(128)S(1)}, s32[2]{0:T(128)}, u32[]{:S(2)}) copy-start(s32[2]{0:T(128)} %param.17) | copy-start | bytes 28
  26.5 16.2 %copy-start.23 = (bf16[4,768,192]{1,2,0:T(8,128)(2,1)S(1)}, bf16[4,768,192]{1,2,0:T(8,128)(2,1)}, u32[]{:S(2)}) copy-start(bf16[4,768,192]{1,2,0:T(8,128)(2,1)} %param.21) | copy-start | bytes 3538948
  29.9 14.7 %copy-start.34 = (f32[2,768]{1,0:T(2,128)}, f32[2,768]{1,0:T(2,128)S(1)}, u32[]{:S(2)}) copy-start(f32[2,768]{1,0:T(2,128)S(1)} %get-tuple-element.80) | copy-start | bytes 18436
  45.4 6.8 %copy-start.12 = (bf16[1,2,256,192]{2,3,0,1:T(8,128)(2,1)}, bf16[1,2,256,192]{2,3,0,1:T(8,128)(2,1)S(1)}, u32[]{:S(2)}) copy-start(bf16[1,2,256,192]{2,3,0,1:T(8,128)(2,1)S(1)} %get-tuple-element.72) | copy-start | bytes 589828
  47.0 3.1 copy-start.17
  47.0 3.1 copy-start.19
  47.0 3.1 copy-start.55
  52.2 3.5 copy-start.28
  55.7 28.0 %copy-start.46 = (f32[2,768]{1,0:T(2,128)S(1)}, f32[2,768]{1,0:T(2,128)}, u32[]{:S(2)}) copy-start(f32[2,768]{1,0:T(2,128)} %get-tuple-element.77) | copy-start | bytes 18436
  57.0 30.4 %copy-start.8 = (bf16[2,64,768]{2,1,0:T(8,128)(2,1)S(1)}, bf16[2,64,768]{2,1,0:T(8,128)(2,1)}, u32[]{:S(2)}) copy-start(bf16[2,64,768]{2,1,0:T(8,128)(2,1)} %param.25) | copy-start | bytes 589828
  57.0 79.3 %reduce-scatter.11.cloned.1.call-start = ((), (), s32[]{:S(2)}) async-start(), calls=%async_computation.10 | async-start | bytes 983040 | tf_op jit(solution)/shard_map/reduce_scatter | solution.py:165
  84.7 1.5 collective-permute-start
  87.1 16.5 %collective-permute-start.1 = (bf16[2,2,64,768]{3,2,1,0:T(8,128)(2,1)}, bf16[2,2,64,768]{3,2,1,0:T(8,128)(2,1)}, u32[]{:S(2)}, u32[]{:S(2)}) collective-permute-start(bf16[2,2,64,768]{3,2,1,0:T(8,128)(2,1)} %pad_maximum_fusion.6), channel_id=1, source_target_pairs={{0,2},{1,3},{2,0},{3,1},{4,6},{5,7},{6,4},{7,5},{8,10},{9,11},{10,... | collective-permute-start | bytes 1179656 | tf_op jit(solution)/shard_map/ppermute | solution.py:25
  103.5 3.8 %copy-start.27 = (bf16[2,256,768]{2,1,0:T(8,128)(2,1)}, bf16[2,256,768]{2,1,0:T(8,128)(2,1)S(1)}, u32[]{:S(2)}) copy-start(bf16[2,256,768]{2,1,0:T(8,128)(2,1)S(1)} %all_gather.13) | copy-start | bytes 2359300
  110.6 25.7 %copy-start.5 = (bf16[2,64,768]{2,1,0:T(8,128)(2,1)S(1)}, bf16[2,64,768]{2,1,0:T(8,128)(2,1)}, u32[]{:S(2)}) copy-start(bf16[2,64,768]{2,1,0:T(8,128)(2,1)} %reduce-scatter.7.cloned.1.call-done) | copy-start | bytes 589828
  110.6 25.7 %copy-start.38 = (f32[2,64]{1,0:T(2,128)S(1)}, f32[2,64]{1,0:T(2,128)}, u32[]{:S(2)}) copy-start(f32[2,64]{1,0:T(2,128)} %copy-done.37) | copy-start | bytes 1540
  110.6 25.7 %copy-start.41 = (f32[2,64]{1,0:T(2,128)S(1)}, f32[2,64]{1,0:T(2,128)}, u32[]{:S(2)}) copy-start(f32[2,64]{1,0:T(2,128)} %copy-done.40) | copy-start | bytes 1540
  112.9 34.5 %copy-start.22 = (f32[2,3,64,256]{3,2,1,0:T(8,128)S(1)}, f32[2,3,64,256]{3,2,1,0:T(8,128)}, u32[]{:S(2)}) copy-start(f32[2,3,64,256]{3,2,1,0:T(8,128)} %copy-done.21) | copy-start | bytes 1179652
  113.0 115.8 %reduce-scatter.13.cloned.1.call-start = ((), (), s32[]{:S(2)}) async-start(), calls=%async_computation.11 | async-start | bytes 983040 | tf_op jit(solution)/shard_map/reduce_scatter | solution.py:216
  154.6 75.1 %reduce-scatter.9.cloned.1.call-start = ((), (), s32[]{:S(2)}) async-start(), calls=%async_computation.9 | async-start | bytes 983040 | tf_op jit(solution)/shard_map/reduce_scatter | solution.py:140
  154.7 3.4 copy-start.15
  158.0 124.7 %reduce-scatter.15.cloned.1.call-start = ((), (), s32[]{:S(2)}) async-start(), calls=%async_computation.12 | async-start | bytes 1658880 | tf_op jit(solution)/shard_map/reduce_scatter | solution.py:283
  172.2 183.8 %reduce-scatter.17.cloned.1.call-start = ((), (), s32[]{:S(2)}) async-start(), calls=%async_computation.13 | async-start | bytes 3981312 | tf_op jit(solution)/shard_map/reduce_scatter | solution.py:283
  184.9 5.4 %copy-start.7 = (bf16[8,576,128]{2,1,0:T(8,128)(2,1)S(1)}, bf16[8,576,128]{2,1,0:T(8,128)(2,1)}, u32[]{:S(2)}) copy-start(bf16[8,576,128]{2,1,0:T(8,128)(2,1)} %reshape.222) | copy-start | bytes 3538948
  194.0 5.3 %copy-start.61 = (s32[2]{0:T(128)S(1)}, s32[2]{0:T(128)}, u32[]{:S(2)}) copy-start(s32[2]{0:T(128)} %param.16) | copy-start | bytes 28
  194.1 5.4 %copy-start.6 = (bf16[2,64,768]{2,1,0:T(8,128)(2,1)S(1)}, bf16[2,64,768]{2,1,0:T(8,128)(2,1)}, u32[]{:S(2)}) copy-start(bf16[2,64,768]{2,1,0:T(8,128)(2,1)} %reduce-scatter.11.cloned.1.call-done) | copy-start | bytes 589828
  195.9 15.7 %all-to-all-start.1 = ((bf16[2,3,256,256]{3,0,1,2:T(2,128)(2,1)}), bf16[2,3,256,256]{3,0,1,2:T(2,128)(2,1)S(1)}, u32[]{:S(2)}, u32[]{:S(2)}) async-start(bf16[2,3,256,256]{3,0,1,2:T(2,128)(2,1)} %copy.106), calls=%async_computation.5 | async-start | bytes 1572864 | tf_op jit(solution)/shard_map/all_to_all | solution.py:224
  211.7 8.4 %copy-start.43 = (bf16[12,256]{1,0:T(8,128)(2,1)S(1)}, bf16[12,256]{1,0:T(8,128)(2,1)}, u32[]{:S(2)}) copy-start(bf16[12,256]{1,0:T(8,128)(2,1)} %param.20) | copy-start | bytes 18436
  220.1 9.7 %copy-start.9 = (bf16[2,64,768]{2,1,0:T(8,128)(2,1)S(1)}, bf16[2,64,768]{2,1,0:T(8,128)(2,1)}, u32[]{:S(2)}) copy-start(bf16[2,64,768]{2,1,0:T(8,128)(2,1)} %param.25) | copy-start | bytes 589828
  220.1 9.7 %copy-start.35 = (f32[2,768]{1,0:T(2,128)S(1)}, f32[2,768]{1,0:T(2,128)}, u32[]{:S(2)}) copy-start(f32[2,768]{1,0:T(2,128)} %copy-done.34) | copy-start | bytes 18436
  220.1 9.7 %copy-start.36 = (f32[2,768]{1,0:T(2,128)S(1)}, f32[2,768]{1,0:T(2,128)}, u32[]{:S(2)}) copy-start(f32[2,768]{1,0:T(2,128)} %get-tuple-element.76) | copy-start | bytes 18436
  220.1 9.7 %copy-start.39 = (f32[2,64]{1,0:T(2,128)S(1)}, f32[2,64]{1,0:T(2,128)}, u32[]{:S(2)}) copy-start(f32[2,64]{1,0:T(2,128)} %copy-done.37) | copy-start | bytes 1540
  220.1 9.7 %copy-start.42 = (f32[2,64]{1,0:T(2,128)S(1)}, f32[2,64]{1,0:T(2,128)}, u32[]{:S(2)}) copy-start(f32[2,64]{1,0:T(2,128)} %copy-done.40) | copy-start | bytes 1540
  220.1 9.7 %copy-start.45 = (f32[2,64]{1,0:T(2,128)S(1)}, f32[2,64]{1,0:T(2,128)}, u32[]{:S(2)}) copy-start(f32[2,64]{1,0:T(2,128)} %copy-done.44) | copy-start | bytes 1540
  220.2 9.7 %copy-start.48 = (f32[2,64]{1,0:T(2,128)S(1)}, f32[2,64]{1,0:T(2,128)}, u32[]{:S(2)}) copy-start(f32[2,64]{1,0:T(2,128)} %copy-done.47) | copy-start | bytes 1540
  220.2 9.7 %copy-start.50 = (f32[2,64]{1,0:T(2,128)S(1)}, f32[2,64]{1,0:T(2,128)}, u32[]{:S(2)}) copy-start(f32[2,64]{1,0:T(2,128)} %copy-done.49) | copy-start | bytes 1540
  220.2 9.7 %copy-start.52 = (f32[2,64]{1,0:T(2,128)S(1)}, f32[2,64]{1,0:T(2,128)}, u32[]{:S(2)}) copy-start(f32[2,64]{1,0:T(2,128)} %copy-done.51) | copy-start | bytes 1540
  232.2 13.2 %copy-start.54 = (f32[2,256]{1,0:T(2,128)S(1)}, f32[2,256]{1,0:T(2,128)}, u32[]{:S(2)}) copy-start(f32[2,256]{1,0:T(2,128)} %copy-done.53) | copy-start | bytes 6148
  278.2 3.5 copy-start.16
  (27 other events, 43.3 us)
Sparse Core Ops, SparseCore 0:
  57.2 24.2 reduce-scatter.6
  113.1 23.1 reduce-scatter.10
  154.7 23.7 reduce-scatter.12
  180.9 23.7 reduce-scatter.8
  208.1 65.7 reduce-scatter.14
  277.4 78.5 reduce-scatter.16
